TPU v7x, 256 devices: a whole 4x4x8 slice. The times are simulated.
256 devices in a mesh: dp: 8 (over x, core), expert: 32 (over y, z).
Axes of the slice: x: 4, y: 4, z: 8, core: 2. Of those that a mesh axis runs over, the one named last changes fastest.
Arguments:
- tokens: bfloat16 [4096, 5120], P('expert', 'dp'), may hold values from -6 to 6
- out_grad: bfloat16 [4096, 5120], P('expert', 'dp'), may hold values from -0.59765625 to 0.59765625
- gate_values: float32 [4096, 8], P('expert'), may hold values from 0.05 to 0.5
- route_lists: int32 [4096, 8], P('expert'), may hold values from 0 to 15, all different within a row; in each aligned block of 128 rows (0 to 127, 128 to 255, ...) at most 72 rows name the same one
- expert_pairs: int32 [16], replicated, may hold values from 0 to 15, as said below
- gate_weight: bfloat16 [32, 5120, 1024], P('expert', 'dp'), as said below
- up_weight: bfloat16 [32, 5120, 1024], P('expert', 'dp'), as said below
- down_weight: bfloat16 [32, 1024, 5120], P('expert', None, 'dp'), as said below
Outputs:
- layer_output: bfloat16 [4096, 5120], P('expert', 'dp')
- token_grad: bfloat16 [4096, 5120], P('expert', 'dp')
- gate_value_grad: float32 [4096, 8], P('expert')
- gate_weight_grad: bfloat16 [32, 5120, 1024], P('expert', 'dp')
- up_weight_grad: bfloat16 [32, 5120, 1024], P('expert', 'dp')
- down_weight_grad: bfloat16 [32, 1024, 5120], P('expert', None, 'dp')
Inputs may be any that keep to these rules, and one draw needn't show every extreme that they name: `route_lists`: each token names 8 different experts; within each aligned block of 128 tokens no expert is named by more than 72 tokens. `expert_pairs`: a permutation; pair p is made of slots p and p + 16. `gate_weight`: slots p and p + 16 hold equal matrices, those of expert expert_pairs[p]. `up_weight`: slots p and p + 16 hold equal matrices. `down_weight`: slots p and p + 16 hold equal matrices.
All inputs are finite; a program needn't handle non-finite values.
Results may differ from a plain program's by a relative error of at most 0.023.
Values may be sent and summed in bfloat16 or wider, within the bound.
A program may use at most 128 MiB of HBM per device.

v0:
```python
import jax
import jax.numpy as jnp
from jax import lax
from jax.sharding import PartitionSpec as P

HALF = 36


def partner(x, axis, distance):
    return lax.ppermute(x, axis, [(i, i ^ 1 << distance) for i in range(lax.axis_size(axis))])


def shards(
    tokens, out_grad, gate_values, route_lists, expert_pairs, gate_weight, up_weight, down_weight
):
    tok_rows, width_dev = tokens.shape
    top_count = route_lists.shape[1]
    slot_count = lax.axis_size("expert")
    pair_count = slot_count // 2
    swap_bit = slot_count.bit_length() - 2
    contract_first = (((0,), (0,)), ((), ()))
    contract_second = (((1,), (1,)), ((), ()))
    catalog = jnp.arange(pair_count, dtype=jnp.int32)
    chosen = (route_lists[:, :, None] == catalog[None, None, :]).astype(jnp.int32)
    present = jnp.sum(chosen, axis=1)
    before = jnp.cumsum(present, axis=0) - present
    position = jnp.sum(chosen * before[:, None, :], axis=2)
    owner_pair = jnp.sum(
        jnp.where(
            route_lists[:, :, None] == expert_pairs[None, None, :], catalog[None, None, :], 0
        ),
        axis=2,
    )
    is_upper = (position >= HALF).astype(jnp.int32)
    target = (owner_pair + pair_count * is_upper) * HALF + position - HALF * is_upper
    capacity = slot_count * HALF
    flat_count = tok_rows * top_count
    slot_table = (
        jnp.full((capacity,), flat_count, jnp.int32)
        .at[target.reshape(-1)]
        .set(jnp.arange(flat_count, dtype=jnp.int32))
    )
    token_of = jnp.where(slot_table < flat_count, slot_table // top_count, tok_rows)
    padded_tokens = jnp.concatenate([tokens, jnp.zeros((1, width_dev), jnp.bfloat16)], axis=0)
    scaled_cot = (
        (gate_values[:, :, None] * out_grad.astype(jnp.float32)[:, None, :])
        .astype(jnp.bfloat16)
        .reshape(flat_count, width_dev)
    )
    padded_cot = jnp.concatenate([scaled_cot, jnp.zeros((1, width_dev), jnp.bfloat16)], axis=0)
    sent_tokens = padded_tokens[token_of].reshape(slot_count, HALF, width_dev)
    sent_cot = padded_cot[slot_table].reshape(slot_count, HALF, width_dev)
    got_tokens, got_cot = (
        lax.all_to_all(sent_tokens, "expert", split_axis=0, concat_axis=0, tiled=True),
        lax.all_to_all(sent_cot, "expert", split_axis=0, concat_axis=0, tiled=True),
    )
    row_total = slot_count * HALF
    rows_in = got_tokens.reshape(row_total, width_dev)
    cot_rows = got_cot.reshape(row_total, width_dev)
    w_gate = gate_weight[0]
    w_up = up_weight[0]
    w_down = down_weight[0]
    part_gate = jnp.dot(rows_in, w_gate, preferred_element_type=jnp.float32)
    part_up = jnp.dot(rows_in, w_up, preferred_element_type=jnp.float32)
    gate_pre, up_pre = (
        lax.psum(part_gate.astype(jnp.bfloat16), "dp").astype(jnp.float32),
        lax.psum(part_up.astype(jnp.bfloat16), "dp").astype(jnp.float32),
    )
    hidden = (jax.nn.silu(gate_pre) * up_pre).astype(jnp.bfloat16)
    expert_out = jnp.dot(hidden, w_down, preferred_element_type=jnp.float32).astype(jnp.bfloat16)
    grad_down = lax.dot_general(
        hidden, cot_rows, contract_first, preferred_element_type=jnp.float32
    ).astype(jnp.bfloat16)
    back_part = lax.dot_general(
        cot_rows, w_down, contract_second, preferred_element_type=jnp.float32
    )
    hidden_grad = lax.psum(back_part.astype(jnp.bfloat16), "dp").astype(jnp.float32)
    sigmoid_gate = jax.nn.sigmoid(gate_pre)
    up_grad = (hidden_grad * gate_pre * sigmoid_gate).astype(jnp.bfloat16)
    pre_grad = (
        hidden_grad * up_pre * sigmoid_gate * (1.0 + gate_pre * (1.0 - sigmoid_gate))
    ).astype(jnp.bfloat16)
    row_input_grad = (
        lax.dot_general(pre_grad, w_gate, contract_second, preferred_element_type=jnp.float32)
        + lax.dot_general(up_grad, w_up, contract_second, preferred_element_type=jnp.float32)
    ).astype(jnp.bfloat16)
    grad_gate = lax.dot_general(
        rows_in, pre_grad, contract_first, preferred_element_type=jnp.float32
    ).astype(jnp.bfloat16)
    grad_up = lax.dot_general(
        rows_in, up_grad, contract_first, preferred_element_type=jnp.float32
    ).astype(jnp.bfloat16)
    partner_gate, partner_up, partner_down = partner(
        (grad_gate, grad_up, grad_down), "expert", swap_bit
    )
    back_out, back_grad = (
        lax.all_to_all(
            expert_out.reshape(slot_count, HALF, width_dev),
            "expert",
            split_axis=0,
            concat_axis=0,
            tiled=True,
        ),
        lax.all_to_all(
            row_input_grad.reshape(slot_count, HALF, width_dev),
            "expert",
            split_axis=0,
            concat_axis=0,
            tiled=True,
        ),
    )
    out_each = back_out.reshape(capacity, width_dev)[target].astype(jnp.float32)
    grad_each = back_grad.reshape(capacity, width_dev)[target].astype(jnp.float32)
    layer_output = jnp.sum(gate_values[:, :, None] * out_each, axis=1).astype(jnp.bfloat16)
    token_grad = jnp.sum(grad_each, axis=1).astype(jnp.bfloat16)
    inner_dots = jnp.sum(out_grad.astype(jnp.float32)[:, None, :] * out_each, axis=2)
    gate_value_grad = lax.psum(inner_dots, "dp")
    gate_weight_grad = (grad_gate.astype(jnp.float32) + partner_gate.astype(jnp.float32)).astype(
        jnp.bfloat16
    )[None]
    up_weight_grad = (grad_up.astype(jnp.float32) + partner_up.astype(jnp.float32)).astype(
        jnp.bfloat16
    )[None]
    down_weight_grad = (grad_down.astype(jnp.float32) + partner_down.astype(jnp.float32)).astype(
        jnp.bfloat16
    )[None]
    return (
        layer_output,
        token_grad,
        gate_value_grad,
        gate_weight_grad,
        up_weight_grad,
        down_weight_grad,
    )


def solution(mesh):
    placed = (
        P("expert", "dp"),
        P("expert", "dp"),
        P("expert", None),
        P("expert", None),
        P(),
        P("expert", "dp", None),
        P("expert", "dp", None),
        P("expert", None, "dp"),
    )
    return jax.shard_map(
        shards,
        mesh=mesh,
        in_specs=placed,
        out_specs=(
            P("expert", "dp"),
            P("expert", "dp"),
            P("expert", None),
            P("expert", "dp", None),
            P("expert", "dp", None),
            P("expert", None, "dp"),
        ),
        check_vma=False,
    )
```

profile of v0, /device:TPU:8, one launch (start us, length us, event | category | flops | bytes accessed | tf_op | source)
XLA Modules:
  0.0 448.8 jit_solution(12803808135160498358)
XLA Ops:
  9.6 4.3 scatter_custom_fusion
  14.9 4.5 %gather_fusion = bf16[1152,640]{1,0:T(8,128)(2,1)S(1)} fusion(bf16[129,640]{1,0:T(8,128)(2,1)S(1)} %concatenate.6, s32[2048]{0:T(1024)S(1)} %get-tuple-element.30), kind=kCustom, calls=%fused_computation | custom fusion | bytes 2953728 | tf_op jit(solution)/shard_map/gather | solution.py:51
  20.7 11.9 %all-to-all-start = ((bf16[32,36,640]{2,1,0:T(8,128)(2,1)}), bf16[32,36,640]{2,1,0:T(8,128)(2,1)}, u32[]{:S(2)}, u32[]{:S(2)}) async-start(bf16[32,36,640]{2,1,0:T(8,128)(2,1)} %reshape.143), calls=%async_computation | async-start | bytes 3276800 | tf_op jit(solution)/shard_map/all_to_all | solution.py:54
  33.2 4.8 %gather_fusion.2 = bf16[1152,640]{1,0:T(8,128)(2,1)} fusion(bf16[1025,640]{1,0:T(8,128)(2,1)S(1)} %concatenate.7, s32[2048]{0:T(1024)S(1)} %get-tuple-element.29), kind=kCustom, calls=%fused_computation.2 | custom fusion | bytes 2953728 | tf_op jit(solution)/shard_map/gather | solution.py:52
  41.3 29.5 %all-to-all-done = bf16[32,36,640]{2,1,0:T(8,128)(2,1)} async-done(((bf16[32,36,640]{2,1,0:T(8,128)(2,1)}), bf16[32,36,640]{2,1,0:T(8,128)(2,1)}, u32[]{:S(2)}, u32[]{:S(2)}) %all-to-all-start) | async-done | bytes 1474592 | tf_op jit(solution)/shard_map/all_to_all | solution.py:54
  70.8 8.2 %all-to-all-start.2 = ((bf16[32,36,640]{2,1,0:T(8,128)(2,1)}), bf16[32,36,640]{2,1,0:T(8,128)(2,1)S(1)}, u32[]{:S(2)}, u32[]{:S(2)}) async-start(bf16[32,36,640]{2,1,0:T(8,128)(2,1)} %reshape.147), calls=%async_computation.2 | async-start | bytes 3276800 | tf_op jit(solution)/shard_map/all_to_all | solution.py:55
  79.2 3.3 reshape.144
  82.6 5.3 %convolution_convert_fusion.1 = bf16[1152,1024]{1,0:T(8,128)(2,1)} fusion(bf16[1152,640]{1,0:T(8,128)(2,1)} %reshape.144, bf16[1,640,1024]{2,1,0:T(8,128)(2,1)} %param.14), kind=kOutput, calls=%fused_computation.22 | convolution fusion | flops 1511129088 | bytes 5144576 | tf_op jit(solution)/shard_map/dot_general | solution.py:64
  87.9 3.5 convolution_convert_fusion.2
  91.4 25.3 %all-to-all-done.2 = bf16[32,36,640]{2,1,0:T(8,128)(2,1)S(1)} async-done(((bf16[32,36,640]{2,1,0:T(8,128)(2,1)}), bf16[32,36,640]{2,1,0:T(8,128)(2,1)S(1)}, u32[]{:S(2)}, u32[]{:S(2)}) %all-to-all-start.2) | async-done | bytes 1474592 | tf_op jit(solution)/shard_map/all_to_all | solution.py:55
  117.9 5.3 %convolution_convert_fusion = bf16[1152,1024]{1,0:T(8,128)(2,1)} fusion(bf16[1152,640]{1,0:T(8,128)(2,1)} %reshape.148, bf16[1,1024,640]{2,1,0:T(8,128)(2,1)} %param.15), kind=kOutput, calls=%fused_computation.21 | convolution fusion | flops 1511129088 | bytes 5144576 | tf_op jit(solution)/shard_map/dot_general | solution.py:74
  123.3 96.2 %all-reduce.5.cloned.1.call-done = (bf16[1152,1024]{1,0:T(8,128)(2,1)}, bf16[1152,1024]{1,0:T(8,128)(2,1)}, bf16[1152,1024]{1,0:T(8,128)(2,1)}) async-done(((bf16[1152,1024]{1,0:T(8,128)(2,1)}, bf16[1152,1024]{1,0:T(8,128)(2,1)}, bf16[1152,1024]{1,0:T(8,128)(2,1)}), (bf16[1152,1024]{1,0:T(8,128)(2,1)}, bf16[1152,1024]{1,0:T(8,128)(2,1)}, bf16[1152,1024]{1,0:T(8,128)(2,1)})) %all-reduce.5.cloned.1.call-update) | async-done | bytes 7077904 | tf_op jit(solution)/shard_map/psum | solution.py:67
  219.4 5.7 %fusion.3 = (bf16[1152,1024]{1,0:T(8,128)(2,1)S(1)}, bf16[1152,1024]{1,0:T(8,128)(2,1)}) fusion(bf16[1152,1024]{1,0:T(8,128)(2,1)} %get-tuple-element.22, bf16[1152,1024]{1,0:T(8,128)(2,1)} %get-tuple-element.24, bf16[1152,1024]{1,0:T(8,128)(2,1)} %get-tuple-element.23), kind=kLoop, calls=%fused_computation.14 | loop fusion | flops 18874368 | bytes 11796480 | tf_op jit(solution)/shard_map/convert_element_type | solution.py:82
  232.9 10.2 %all-to-all-start.3 = ((bf16[32,36,640]{2,1,0:T(8,128)(2,1)}), bf16[32,36,640]{2,1,0:T(8,128)(2,1)S(1)}, u32[]{:S(2)}, u32[]{:S(2)}) async-start(bf16[32,36,640]{2,1,0:T(8,128)(2,1)} %reshape.149), calls=%async_computation.3 | async-start | bytes 3276800 | tf_op jit(solution)/shard_map/all_to_all | solution.py:104
  243.1 4.0 convolution_convert_fusion.3
  248.5 32.7 %all-to-all-done.3 = bf16[32,36,640]{2,1,0:T(8,128)(2,1)S(1)} async-done(((bf16[32,36,640]{2,1,0:T(8,128)(2,1)}), bf16[32,36,640]{2,1,0:T(8,128)(2,1)S(1)}, u32[]{:S(2)}, u32[]{:S(2)}) %all-to-all-start.3) | async-done | bytes 1474592 | tf_op jit(solution)/shard_map/all_to_all | solution.py:104
  281.2 8.0 %all-to-all-start.1 = ((bf16[32,36,640]{2,1,0:T(8,128)(2,1)}), bf16[32,36,640]{2,1,0:T(8,128)(2,1)}, u32[]{:S(2)}, u32[]{:S(2)}) async-start(bf16[32,36,640]{2,1,0:T(8,128)(2,1)} %reshape.145), calls=%async_computation.1 | async-start | bytes 3276800 | tf_op jit(solution)/shard_map/all_to_all | solution.py:97
  289.2 5.6 %convolution_convert_fusion.5 = bf16[640,1024]{1,0:T(8,128)(2,1)} fusion(bf16[1152,640]{1,0:T(8,128)(2,1)S(1)} %copy-done.8, bf16[1152,1024]{1,0:T(8,128)(2,1)} %get-tuple-element.23, bf16[1152,1024]{1,0:T(8,128)(2,1)} %get-tuple-element.24), kind=kOutput, calls=%fused_computation.37 | convolution fusion | flops 1520041984 | bytes 7503872 | tf_op jit(solution)/shard_map/dot_general | solution.py:90
  306.2 34.9 %collective-permute-done.1 = bf16[640,1024]{1,0:T(8,128)(2,1)} collective-permute-done((bf16[640,1024]{1,0:T(8,128)(2,1)}, bf16[640,1024]{1,0:T(8,128)(2,1)}, u32[]{:S(2)}, u32[]{:S(2)}) %collective-permute-start.1) | collective-permute-done | bytes 1310752 | tf_op jit(solution)/shard_map/ppermute | solution.py:10
  344.4 24.8 %collective-permute-done = bf16[640,1024]{1,0:T(8,128)(2,1)} collective-permute-done((bf16[640,1024]{1,0:T(8,128)(2,1)}, bf16[640,1024]{1,0:T(8,128)(2,1)}, u32[]{:S(2)}, u32[]{:S(2)}) %collective-permute-start) | collective-permute-done | bytes 1310752 | tf_op jit(solution)/shard_map/ppermute | solution.py:10
  372.5 23.8 %collective-permute-done.2 = bf16[1024,640]{1,0:T(8,128)(2,1)} collective-permute-done((bf16[1024,640]{1,0:T(8,128)(2,1)S(1)}, bf16[1024,640]{1,0:T(8,128)(2,1)}, u32[]{:S(2)}, u32[]{:S(2)}) %collective-permute-start.2) | collective-permute-done | bytes 1310752 | tf_op jit(solution)/shard_map/ppermute | solution.py:10
  399.3 4.0 gather_fusion.3
  407.2 5.1 %gather_fusion.1 = bf16[1024,640]{1,0:T(8,128)(2,1)} fusion(bf16[1152,640]{1,0:T(8,128)(2,1)S(1)} %reshape.146, s32[1024]{0:T(1024)S(1)} %broadcast_clamp_fusion), kind=kCustom, calls=%fused_computation.1 | custom fusion | bytes 2625536 | tf_op jit(solution)/shard_map/gather | solution.py:112
  415.6 25.7 %psum.31 = f32[128,8]{1,0:T(8,128)S(1)} all-reduce(f32[128,8]{1,0:T(8,128)S(1)} %get-tuple-element.18), channel_id=1, replica_groups=mesh['dp'=8,'expert'=32] {'dp'}, use_global_device_ids=true, to_apply=%region_11.12 | all-reduce | flops 1024 | bytes 8192 | tf_op jit(solution)/shard_map/psum | solution.py:117
  (73 shorter events, 47.9 us)
Async XLA Ops:
  7.2 80.7 %copy-start = (bf16[1,640,1024]{2,1,0:T(8,128)(2,1)S(1)}, bf16[1,640,1024]{2,1,0:T(8,128)(2,1)}, u32[]{:S(2)}) copy-start(bf16[1,640,1024]{2,1,0:T(8,128)(2,1)} %param.13) | copy-start | bytes 3932164
  20.7 11.9 %copy-start.11 = (f32[128,8]{0,1:T(8,128)S(1)}, f32[128,8]{0,1:T(8,128)}, u32[]{:S(2)}) copy-start(f32[128,8]{0,1:T(8,128)} %param.10) | copy-start | bytes 12292
  20.7 12.1 %copy-start.10 = (bf16[128,640]{1,0:T(8,128)(2,1)S(1)}, bf16[128,640]{1,0:T(8,128)(2,1)}, u32[]{:S(2)}) copy-start(bf16[128,640]{1,0:T(8,128)(2,1)} %param.9) | copy-start | bytes 491524
  20.7 50.1 %all-to-all-start = ((bf16[32,36,640]{2,1,0:T(8,128)(2,1)}), bf16[32,36,640]{2,1,0:T(8,128)(2,1)}, u32[]{:S(2)}, u32[]{:S(2)}) async-start(bf16[32,36,640]{2,1,0:T(8,128)(2,1)} %reshape.143), calls=%async_computation | async-start | bytes 3276800 | tf_op jit(solution)/shard_map/all_to_all | solution.py:54
  70.8 45.9 %all-to-all-start.2 = ((bf16[32,36,640]{2,1,0:T(8,128)(2,1)}), bf16[32,36,640]{2,1,0:T(8,128)(2,1)S(1)}, u32[]{:S(2)}, u32[]{:S(2)}) async-start(bf16[32,36,640]{2,1,0:T(8,128)(2,1)} %reshape.147), calls=%async_computation.2 | async-start | bytes 3276800 | tf_op jit(solution)/shard_map/all_to_all | solution.py:55
  79.0 140.4 %all-reduce.5.cloned.1.call-start = ((), (), s32[]{:S(2)}) async-start(), calls=%async_computation.4 | async-start | bytes 14155776 | tf_op jit(solution)/shard_map/psum | solution.py:67
  82.6 5.3 %copy-start.7 = (bf16[1152,640]{1,0:T(8,128)(2,1)S(1)}, bf16[1152,640]{1,0:T(8,128)(2,1)}, u32[]{:S(2)}) copy-start(bf16[1152,640]{1,0:T(8,128)(2,1)} %reshape.144) | copy-start | bytes 4423684
  225.1 1.5 copy-start.5
  226.6 2.0 copy-start.2
  226.6 2.4 copy-start.3
  226.6 2.7 copy-start.12
  232.9 48.2 %all-to-all-start.3 = ((bf16[32,36,640]{2,1,0:T(8,128)(2,1)}), bf16[32,36,640]{2,1,0:T(8,128)(2,1)S(1)}, u32[]{:S(2)}, u32[]{:S(2)}) async-start(bf16[32,36,640]{2,1,0:T(8,128)(2,1)} %reshape.149), calls=%async_computation.3 | async-start | bytes 3276800 | tf_op jit(solution)/shard_map/all_to_all | solution.py:104
  248.5 40.7 %copy-start.8 = (bf16[1152,640]{1,0:T(8,128)(2,1)S(1)}, bf16[1152,640]{1,0:T(8,128)(2,1)}, u32[]{:S(2)}) copy-start(bf16[1152,640]{1,0:T(8,128)(2,1)} %reshape.144) | copy-start | bytes 4423684
  281.2 123.7 %all-to-all-start.1 = ((bf16[32,36,640]{2,1,0:T(8,128)(2,1)}), bf16[32,36,640]{2,1,0:T(8,128)(2,1)}, u32[]{:S(2)}, u32[]{:S(2)}) async-start(bf16[32,36,640]{2,1,0:T(8,128)(2,1)} %reshape.145), calls=%async_computation.1 | async-start | bytes 3276800 | tf_op jit(solution)/shard_map/all_to_all | solution.py:97
  289.2 7.7 %copy-start.6 = (bf16[1152,1024]{1,0:T(8,128)(2,1)S(1)}, bf16[1152,1024]{1,0:T(8,128)(2,1)}, u32[]{:S(2)}) copy-start(bf16[1152,1024]{1,0:T(8,128)(2,1)} %copy-done.5) | copy-start | bytes 7077892
  294.8 6.5 %copy-start.4 = (bf16[1152,1024]{1,0:T(8,128)(2,1)S(1)}, bf16[1152,1024]{1,0:T(8,128)(2,1)}, u32[]{:S(2)}) copy-start(bf16[1152,1024]{1,0:T(8,128)(2,1)} %get-tuple-element.26) | copy-start | bytes 7077892
  294.8 6.5 %copy-start.9 = (bf16[1152,640]{1,0:T(8,128)(2,1)S(1)}, bf16[1152,640]{1,0:T(8,128)(2,1)}, u32[]{:S(2)}) copy-start(bf16[1152,640]{1,0:T(8,128)(2,1)} %reshape.148) | copy-start | bytes 4423684
  294.8 46.3 %collective-permute-start.1 = (bf16[640,1024]{1,0:T(8,128)(2,1)}, bf16[640,1024]{1,0:T(8,128)(2,1)}, u32[]{:S(2)}, u32[]{:S(2)}) collective-permute-start(bf16[640,1024]{1,0:T(8,128)(2,1)} %convolution_convert_fusion.5), channel_id=1, source_target_pairs={{0,16},{1,17},{2,18},{3,19},{4,20},{5,21},{6,22},{7,23},{8,24},{9,... | collective-permute-start | bytes 3932168 | tf_op jit(solution)/shard_map/ppermute | solution.py:10
  299.9 69.3 %collective-permute-start = (bf16[640,1024]{1,0:T(8,128)(2,1)}, bf16[640,1024]{1,0:T(8,128)(2,1)}, u32[]{:S(2)}, u32[]{:S(2)}) collective-permute-start(bf16[640,1024]{1,0:T(8,128)(2,1)} %convolution_convert_fusion.6), channel_id=1, source_target_pairs={{0,16},{1,17},{2,18},{3,19},{4,20},{5,21},{6,22},{7,23},{8,24},{9,... | collective-permute-start | bytes 3932168 | tf_op jit(solution)/shard_map/ppermute | solution.py:10
  303.5 92.8 %collective-permute-start.2 = (bf16[1024,640]{1,0:T(8,128)(2,1)S(1)}, bf16[1024,640]{1,0:T(8,128)(2,1)}, u32[]{:S(2)}, u32[]{:S(2)}) collective-permute-start(bf16[1024,640]{1,0:T(8,128)(2,1)S(1)} %convolution_convert_fusion.4), channel_id=1, source_target_pairs={{0,16},{1,17},{2,18},{3,19},{4,20},{5,21},{6,22},{7,23},{8,24},{9,... | collective-permute-start | bytes 3932168 | tf_op jit(solution)/shard_map/ppermute | solution.py:10
  407.2 34.8 %copy-start.1 = (bf16[1,640,1024]{2,1,0:T(8,128)(2,1)S(1)}, bf16[1,640,1024]{2,1,0:T(8,128)(2,1)}, u32[]{:S(2)}) copy-start(bf16[1,640,1024]{2,1,0:T(8,128)(2,1)} %param.13) | copy-start | bytes 3932164
Sparse Core Ops, SparseCore 0:
  123.4 96.0 all-reduce.4
where the time goes:
time: 450 us; the launch traced here: 449 us
  waiting for transfers between devices  267 us (59%)
  starting transfers between devices  44.4 us (10%)
  local copies, waits for them, and re-layouts  42.1 us (9%)
  matrix products  33.2 us (7%)
  blocking collectives  25.7 us (6%)
  other arithmetic  21.9 us (5%)
  between operations  14.3 us (3%)
    psum x1, waiting for transfers between devices, shards(): lax.psum(part_up.astype(jnp.bfloat16), 'dp').astype(jnp.float32)  96.2 us
    ppermute x3, waiting for transfers between devices, partner(): lax.ppermute(x, axis, [(i, i ^ 1 << distance) for i in range(lax.axis_siz...  83.5 us
    all_to_all x1, waiting for transfers between devices, shards(): lax.all_to_all(row_input_grad.reshape(slot_count, HALF, width_dev), 'expe...  32.7 us
    all_to_all x1, waiting for transfers between devices, shards(): lax.all_to_all(sent_tokens, 'expert', split_axis=0, concat_axis=0, tiled=...  29.5 us
    psum x1, blocking collectives, shards(): gate_value_grad = lax.psum(inner_dots, 'dp')  25.7 us
    all_to_all x1, waiting for transfers between devices, shards(): lax.all_to_all(sent_cot, 'expert', split_axis=0, concat_axis=0, tiled=True)  25.3 us
    all_to_all x1, starting transfers between devices, shards(): lax.all_to_all(sent_tokens, 'expert', split_axis=0, concat_axis=0, tiled=...  11.9 us
    all_to_all x1, starting transfers between devices, shards(): lax.all_to_all(row_input_grad.reshape(slot_count, HALF, width_dev), 'expe...  10.2 us
  transfers between devices with their start and end apart: 8, of which 7 were waited for; matrix products, arithmetic and copies ran while one was open for 12% of the time, Pallas kernels for 0%

commit v1 on v0

--- a/solution.py
+++ b/solution.py
@@ -114,7 +114,11 @@
     layer_output = jnp.sum(gate_values[:, :, None] * out_each, axis=1).astype(jnp.bfloat16)
     token_grad = jnp.sum(grad_each, axis=1).astype(jnp.bfloat16)
     inner_dots = jnp.sum(out_grad.astype(jnp.float32)[:, None, :] * out_each, axis=2)
-    gate_value_grad = lax.psum(inner_dots, "dp")
+    gate_value_grad = inner_dots
+    for hop in (1, 2, 4):
+        gate_value_grad = gate_value_grad + lax.ppermute(
+            gate_value_grad, "dp", [(dev, dev ^ hop) for dev in range(8)]
+        )
     gate_weight_grad = (grad_gate.astype(jnp.float32) + partner_gate.astype(jnp.float32)).astype(
         jnp.bfloat16
     )[None]

time: 450 us -> 419 us (0.931)
  blocking collectives: 25.7 us -> 0 us
  waiting for transfers between devices: 267 us -> 256 us
  starting transfers between devices: 44.4 us -> 50.4 us
    all_to_all x1, waiting for transfers between devices: 32.7 us -> 0.01 us  [shards(): lax.all_to_all(row_input_grad.reshape(slot_count, HALF, width_dev), 'expe...]
    all_to_all x1, waiting for transfers between devices: 0.01 us -> 30.6 us  [shards(): lax.all_to_all(expert_out.reshape(slot_count, HALF, width_dev), 'expert',...]
    psum x1 -> x0, blocking collectives: 25.7 us -> none  [shards(): gate_value_grad = lax.psum(inner_dots, 'dp')]
    ppermute x3, waiting for transfers between devices: 83.5 us -> 74.3 us  [partner(): lax.ppermute(x, axis, [(i, i ^ 1 << distance) for i in range(lax.axis_siz...]
    ppermute x0 -> x3, starting transfers between devices: none -> 6.17 us  [shards(): lax.ppermute(gate_value_grad, 'dp', [(dev, dev ^ hop) for dev in range(8)])]
  transfers between devices with their start and end apart: 8 -> 11, of which waited for: 7 -> 7; matrix products, arithmetic and copies ran while one was open for 12% -> 16% of each run, Pallas kernels for 0% -> 0%
where the time goes in v1:
time: 419 us; the launch traced here: 418 us
  waiting for transfers between devices  256 us (61%)
  starting transfers between devices  50.4 us (12%)
  local copies, waits for them, and re-layouts  41.5 us (10%)
  matrix products  33.7 us (8%)
  other arithmetic  22.2 us (5%)
  between operations  14.3 us (3%)
    psum x1, waiting for transfers between devices, shards(): lax.psum(part_up.astype(jnp.bfloat16), 'dp').astype(jnp.float32)  96.2 us
    ppermute x3, waiting for transfers between devices, partner(): lax.ppermute(x, axis, [(i, i ^ 1 << distance) for i in range(lax.axis_siz...  74.3 us
    all_to_all x1, waiting for transfers between devices, shards(): lax.all_to_all(expert_out.reshape(slot_count, HALF, width_dev), 'expert',...  30.6 us
    all_to_all x1, waiting for transfers between devices, shards(): lax.all_to_all(sent_tokens, 'expert', split_axis=0, concat_axis=0, tiled=...  29.5 us
    all_to_all x1, waiting for transfers between devices, shards(): lax.all_to_all(sent_cot, 'expert', split_axis=0, concat_axis=0, tiled=True)  25.3 us
    all_to_all x1, starting transfers between devices, shards(): lax.all_to_all(sent_tokens, 'expert', split_axis=0, concat_axis=0, tiled=...  11.9 us
    all_to_all x1, starting transfers between devices, shards(): lax.all_to_all(expert_out.reshape(slot_count, HALF, width_dev), 'expert',...  10.3 us
  transfers between devices with their start and end apart: 11, of which 7 were waited for; matrix products, arithmetic and copies ran while one was open for 16% of the time, Pallas kernels for 0%

profile of v1, /device:TPU:8, one launch (start us, length us, event | category | flops | bytes accessed | tf_op | source)
XLA Modules:
  0.0 418.1 jit_solution(9133412958255246245)
XLA Ops:
  9.6 4.3 %scatter_custom_fusion = s32[1152]{0:T(1024)S(1)} fusion(s32[1024]{0:T(1024)S(1)} %bitcast.60, s32[1024]{0:T(1024)S(1)} %iota.7, s32[]{:T(128)} %constant.16.clone.1), kind=kCustom, calls=%fused_computation.77 | custom fusion | bytes 4612 | tf_op jit(solution)/shard_map/scatter | solution.py:41
  14.9 4.5 %gather_fusion = bf16[1152,640]{1,0:T(8,128)(2,1)S(1)} fusion(bf16[129,640]{1,0:T(8,128)(2,1)S(1)} %concatenate.6, s32[2048]{0:T(1024)S(1)} %get-tuple-element.30), kind=kCustom, calls=%fused_computation | custom fusion | bytes 2953728 | tf_op jit(solution)/shard_map/gather | solution.py:51
  20.7 11.9 %all-to-all-start = ((bf16[32,36,640]{2,1,0:T(8,128)(2,1)}), bf16[32,36,640]{2,1,0:T(8,128)(2,1)}, u32[]{:S(2)}, u32[]{:S(2)}) async-start(bf16[32,36,640]{2,1,0:T(8,128)(2,1)} %reshape.143), calls=%async_computation | async-start | bytes 3276800 | tf_op jit(solution)/shard_map/all_to_all | solution.py:54
  33.2 4.8 %gather_fusion.2 = bf16[1152,640]{1,0:T(8,128)(2,1)} fusion(bf16[1025,640]{1,0:T(8,128)(2,1)S(1)} %concatenate.7, s32[2048]{0:T(1024)S(1)} %get-tuple-element.29), kind=kCustom, calls=%fused_computation.2 | custom fusion | bytes 2953728 | tf_op jit(solution)/shard_map/gather | solution.py:52
  41.3 29.5 %all-to-all-done = bf16[32,36,640]{2,1,0:T(8,128)(2,1)} async-done(((bf16[32,36,640]{2,1,0:T(8,128)(2,1)}), bf16[32,36,640]{2,1,0:T(8,128)(2,1)}, u32[]{:S(2)}, u32[]{:S(2)}) %all-to-all-start) | async-done | bytes 1474592 | tf_op jit(solution)/shard_map/all_to_all | solution.py:54
  70.8 8.2 %all-to-all-start.2 = ((bf16[32,36,640]{2,1,0:T(8,128)(2,1)}), bf16[32,36,640]{2,1,0:T(8,128)(2,1)S(1)}, u32[]{:S(2)}, u32[]{:S(2)}) async-start(bf16[32,36,640]{2,1,0:T(8,128)(2,1)} %reshape.147), calls=%async_computation.2 | async-start | bytes 3276800 | tf_op jit(solution)/shard_map/all_to_all | solution.py:55
  79.2 3.3 reshape.144
  82.6 5.4 %convolution_convert_fusion.1 = bf16[1152,1024]{1,0:T(8,128)(2,1)} fusion(bf16[1152,640]{1,0:T(8,128)(2,1)} %reshape.144, bf16[1,640,1024]{2,1,0:T(8,128)(2,1)} %param.14), kind=kOutput, calls=%fused_computation.22 | convolution fusion | flops 1511129088 | bytes 5144576 | tf_op jit(solution)/shard_map/dot_general | solution.py:64
  87.9 3.5 convolution_convert_fusion.2
  91.4 25.3 %all-to-all-done.2 = bf16[32,36,640]{2,1,0:T(8,128)(2,1)S(1)} async-done(((bf16[32,36,640]{2,1,0:T(8,128)(2,1)}), bf16[32,36,640]{2,1,0:T(8,128)(2,1)S(1)}, u32[]{:S(2)}, u32[]{:S(2)}) %all-to-all-start.2) | async-done | bytes 1474592 | tf_op jit(solution)/shard_map/all_to_all | solution.py:55
  118.0 4.9 %convolution_convert_fusion = bf16[1152,1024]{1,0:T(8,128)(2,1)} fusion(bf16[1152,640]{1,0:T(8,128)(2,1)} %reshape.148, bf16[1,1024,640]{2,1,0:T(8,128)(2,1)S(1)} %copy-done), kind=kOutput, calls=%fused_computation.21 | convolution fusion | flops 1511129088 | bytes 5144576 | tf_op jit(solution)/shard_map/dot_general | solution.py:74
  122.9 96.2 %all-reduce.5.cloned.1.call-done = (bf16[1152,1024]{1,0:T(8,128)(2,1)}, bf16[1152,1024]{1,0:T(8,128)(2,1)}, bf16[1152,1024]{1,0:T(8,128)(2,1)}) async-done(((bf16[1152,1024]{1,0:T(8,128)(2,1)}, bf16[1152,1024]{1,0:T(8,128)(2,1)}, bf16[1152,1024]{1,0:T(8,128)(2,1)}), (bf16[1152,1024]{1,0:T(8,128)(2,1)}, bf16[1152,1024]{1,0:T(8,128)(2,1)}, bf16[1152,1024]{1,0:T(8,128)(2,1)})) %all-reduce.5.cloned.1.call-update) | async-done | bytes 7077904 | tf_op jit(solution)/shard_map/psum | solution.py:67
  219.0 5.7 %fusion.3 = (bf16[1152,1024]{1,0:T(8,128)(2,1)}, bf16[1152,1024]{1,0:T(8,128)(2,1)S(1)}) fusion(bf16[1152,1024]{1,0:T(8,128)(2,1)} %get-tuple-element.22, bf16[1152,1024]{1,0:T(8,128)(2,1)} %get-tuple-element.24, bf16[1152,1024]{1,0:T(8,128)(2,1)} %get-tuple-element.23), kind=kLoop, calls=%fused_computation.14 | loop fusion | flops 18874368 | bytes 11796480 | tf_op jit(solution)/shard_map/convert_element_type | solution.py:82
  229.6 10.3 %all-to-all-start.1 = ((bf16[32,36,640]{2,1,0:T(8,128)(2,1)}), bf16[32,36,640]{2,1,0:T(8,128)(2,1)S(1)}, u32[]{:S(2)}, u32[]{:S(2)}) async-start(bf16[32,36,640]{2,1,0:T(8,128)(2,1)} %reshape.145), calls=%async_computation.1 | async-start | bytes 3276800 | tf_op jit(solution)/shard_map/all_to_all | solution.py:97
  239.9 3.8 fusion.21
  247.4 30.6 %all-to-all-done.1 = bf16[32,36,640]{2,1,0:T(8,128)(2,1)S(1)} async-done(((bf16[32,36,640]{2,1,0:T(8,128)(2,1)}), bf16[32,36,640]{2,1,0:T(8,128)(2,1)S(1)}, u32[]{:S(2)}, u32[]{:S(2)}) %all-to-all-start.1) | async-done | bytes 1474592 | tf_op jit(solution)/shard_map/all_to_all | solution.py:97
  278.0 8.0 %all-to-all-start.3 = ((bf16[32,36,640]{2,1,0:T(8,128)(2,1)}), bf16[32,36,640]{2,1,0:T(8,128)(2,1)}, u32[]{:S(2)}, u32[]{:S(2)}) async-start(bf16[32,36,640]{2,1,0:T(8,128)(2,1)} %reshape.149), calls=%async_computation.3 | async-start | bytes 3276800 | tf_op jit(solution)/shard_map/all_to_all | solution.py:104
  286.0 5.6 %convolution_convert_fusion.5 = bf16[640,1024]{1,0:T(8,128)(2,1)} fusion(bf16[1152,640]{1,0:T(8,128)(2,1)S(1)} %copy-done.8, bf16[1152,1024]{1,0:T(8,128)(2,1)} %get-tuple-element.23, bf16[1152,1024]{1,0:T(8,128)(2,1)} %get-tuple-element.24), kind=kOutput, calls=%fused_computation.37 | convolution fusion | flops 1520041984 | bytes 7503872 | tf_op jit(solution)/shard_map/dot_general | solution.py:90
  303.8 34.2 %collective-permute-done.4 = bf16[640,1024]{1,0:T(8,128)(2,1)} collective-permute-done((bf16[640,1024]{1,0:T(8,128)(2,1)}, bf16[640,1024]{1,0:T(8,128)(2,1)}, u32[]{:S(2)}, u32[]{:S(2)}) %collective-permute-start.4) | collective-permute-done | bytes 1310752 | tf_op jit(solution)/shard_map/ppermute | solution.py:10
  341.5 4.0 gather_fusion.1
  347.4 18.6 %collective-permute-done.3 = bf16[640,1024]{1,0:T(8,128)(2,1)} collective-permute-done((bf16[640,1024]{1,0:T(8,128)(2,1)}, bf16[640,1024]{1,0:T(8,128)(2,1)}, u32[]{:S(2)}, u32[]{:S(2)}) %collective-permute-start.3) | collective-permute-done | bytes 1310752 | tf_op jit(solution)/shard_map/ppermute | solution.py:10
  371.5 21.6 %collective-permute-done.5 = bf16[1024,640]{1,0:T(8,128)(2,1)} collective-permute-done((bf16[1024,640]{1,0:T(8,128)(2,1)}, bf16[1024,640]{1,0:T(8,128)(2,1)}, u32[]{:S(2)}, u32[]{:S(2)}) %collective-permute-start.5) | collective-permute-done | bytes 1310752 | tf_op jit(solution)/shard_map/ppermute | solution.py:10
  398.5 5.2 %gather_fusion.3 = bf16[1024,640]{1,0:T(8,128)(2,1)} fusion(bf16[1152,640]{1,0:T(8,128)(2,1)S(1)} %reshape.150, s32[1024]{0:T(1024)S(1)} %broadcast_clamp_fusion), kind=kCustom, calls=%fused_computation.3 | custom fusion | bytes 2625536 | tf_op jit(solution)/shard_map/gather | solution.py:113
  403.7 3.9 collective-permute-start.2
  (85 shorter events, 50.5 us)
Async XLA Ops:
  7.2 110.8 %copy-start = (bf16[1,1024,640]{2,1,0:T(8,128)(2,1)S(1)}, bf16[1,1024,640]{2,1,0:T(8,128)(2,1)}, u32[]{:S(2)}) copy-start(bf16[1,1024,640]{2,1,0:T(8,128)(2,1)} %param.15) | copy-start | bytes 3932164
  20.7 11.9 %copy-start.11 = (f32[128,8]{0,1:T(8,128)S(1)}, f32[128,8]{0,1:T(8,128)}, u32[]{:S(2)}) copy-start(f32[128,8]{0,1:T(8,128)} %param.10) | copy-start | bytes 12292
  20.7 12.1 %copy-start.10 = (bf16[128,640]{1,0:T(8,128)(2,1)S(1)}, bf16[128,640]{1,0:T(8,128)(2,1)}, u32[]{:S(2)}) copy-start(bf16[128,640]{1,0:T(8,128)(2,1)} %param.9) | copy-start | bytes 491524
  20.7 50.1 %all-to-all-start = ((bf16[32,36,640]{2,1,0:T(8,128)(2,1)}), bf16[32,36,640]{2,1,0:T(8,128)(2,1)}, u32[]{:S(2)}, u32[]{:S(2)}) async-start(bf16[32,36,640]{2,1,0:T(8,128)(2,1)} %reshape.143), calls=%async_computation | async-start | bytes 3276800 | tf_op jit(solution)/shard_map/all_to_all | solution.py:54
  70.8 45.9 %all-to-all-start.2 = ((bf16[32,36,640]{2,1,0:T(8,128)(2,1)}), bf16[32,36,640]{2,1,0:T(8,128)(2,1)S(1)}, u32[]{:S(2)}, u32[]{:S(2)}) async-start(bf16[32,36,640]{2,1,0:T(8,128)(2,1)} %reshape.147), calls=%async_computation.2 | async-start | bytes 3276800 | tf_op jit(solution)/shard_map/all_to_all | solution.py:55
  79.0 140.0 %all-reduce.5.cloned.1.call-start = ((), (), s32[]{:S(2)}) async-start(), calls=%async_computation.4 | async-start | bytes 14155776 | tf_op jit(solution)/shard_map/psum | solution.py:67
  82.6 5.4 %copy-start.7 = (bf16[1152,640]{1,0:T(8,128)(2,1)S(1)}, bf16[1152,640]{1,0:T(8,128)(2,1)}, u32[]{:S(2)}) copy-start(bf16[1152,640]{1,0:T(8,128)(2,1)} %reshape.144) | copy-start | bytes 4423684
  82.6 5.4 %copy-start.12 = (bf16[1,640,1024]{2,1,0:T(8,128)(2,1)S(1)}, bf16[1,640,1024]{2,1,0:T(8,128)(2,1)}, u32[]{:S(2)}) copy-start(bf16[1,640,1024]{2,1,0:T(8,128)(2,1)} %param.13) | copy-start | bytes 3932164
  229.6 10.3 %copy-start.13 = (bf16[1,640,1024]{2,1,0:T(8,128)(2,1)S(1)}, bf16[1,640,1024]{2,1,0:T(8,128)(2,1)}, u32[]{:S(2)}) copy-start(bf16[1,640,1024]{2,1,0:T(8,128)(2,1)} %param.13) | copy-start | bytes 3932164
  229.6 48.4 %all-to-all-start.1 = ((bf16[32,36,640]{2,1,0:T(8,128)(2,1)}), bf16[32,36,640]{2,1,0:T(8,128)(2,1)S(1)}, u32[]{:S(2)}, u32[]{:S(2)}) async-start(bf16[32,36,640]{2,1,0:T(8,128)(2,1)} %reshape.145), calls=%async_computation.1 | async-start | bytes 3276800 | tf_op jit(solution)/shard_map/all_to_all | solution.py:97
  239.9 3.9 copy-start.2
  239.9 3.9 copy-start.3
  247.4 38.6 %copy-start.8 = (bf16[1152,640]{1,0:T(8,128)(2,1)S(1)}, bf16[1152,640]{1,0:T(8,128)(2,1)}, u32[]{:S(2)}) copy-start(bf16[1152,640]{1,0:T(8,128)(2,1)} %reshape.144) | copy-start | bytes 4423684
  278.0 118.2 %all-to-all-start.3 = ((bf16[32,36,640]{2,1,0:T(8,128)(2,1)}), bf16[32,36,640]{2,1,0:T(8,128)(2,1)}, u32[]{:S(2)}, u32[]{:S(2)}) async-start(bf16[32,36,640]{2,1,0:T(8,128)(2,1)} %reshape.149), calls=%async_computation.3 | async-start | bytes 3276800 | tf_op jit(solution)/shard_map/all_to_all | solution.py:104
  286.0 7.7 %copy-start.6 = (bf16[1152,1024]{1,0:T(8,128)(2,1)S(1)}, bf16[1152,1024]{1,0:T(8,128)(2,1)}, u32[]{:S(2)}) copy-start(bf16[1152,1024]{1,0:T(8,128)(2,1)} %get-tuple-element.25) | copy-start | bytes 7077892
  291.6 6.5 %copy-start.5 = (bf16[1152,1024]{1,0:T(8,128)(2,1)S(1)}, bf16[1152,1024]{1,0:T(8,128)(2,1)}, u32[]{:S(2)}) copy-start(bf16[1152,1024]{1,0:T(8,128)(2,1)} %copy-done.4) | copy-start | bytes 7077892
  291.6 6.5 %copy-start.9 = (bf16[1152,640]{1,0:T(8,128)(2,1)S(1)}, bf16[1152,640]{1,0:T(8,128)(2,1)}, u32[]{:S(2)}) copy-start(bf16[1152,640]{1,0:T(8,128)(2,1)} %reshape.148) | copy-start | bytes 4423684
  291.6 46.3 %collective-permute-start.4 = (bf16[640,1024]{1,0:T(8,128)(2,1)}, bf16[640,1024]{1,0:T(8,128)(2,1)}, u32[]{:S(2)}, u32[]{:S(2)}) collective-permute-start(bf16[640,1024]{1,0:T(8,128)(2,1)} %convolution_convert_fusion.5), channel_id=1, source_target_pairs={{0,16},{1,17},{2,18},{3,19},{4,20},{5,21},{6,22},{7,23},{8,24},{9,... | collective-permute-start | bytes 3932168 | tf_op jit(solution)/shard_map/ppermute | solution.py:10
  296.7 69.3 %collective-permute-start.3 = (bf16[640,1024]{1,0:T(8,128)(2,1)}, bf16[640,1024]{1,0:T(8,128)(2,1)}, u32[]{:S(2)}, u32[]{:S(2)}) collective-permute-start(bf16[640,1024]{1,0:T(8,128)(2,1)} %convolution_convert_fusion.6), channel_id=1, source_target_pairs={{0,16},{1,17},{2,18},{3,19},{4,20},{5,21},{6,22},{7,23},{8,24},{9,... | collective-permute-start | bytes 3932168 | tf_op jit(solution)/shard_map/ppermute | solution.py:10
  301.4 91.7 %collective-permute-start.5 = (bf16[1024,640]{1,0:T(8,128)(2,1)}, bf16[1024,640]{1,0:T(8,128)(2,1)}, u32[]{:S(2)}, u32[]{:S(2)}) collective-permute-start(bf16[1024,640]{1,0:T(8,128)(2,1)} %convolution_convert_fusion.4), channel_id=1, source_target_pairs={{0,16},{1,17},{2,18},{3,19},{4,20},{5,21},{6,22},{7,23},{8,24},{9,... | collective-permute-start | bytes 3932168 | tf_op jit(solution)/shard_map/ppermute | solution.py:10
  347.4 21.9 %collective-permute-start = (f32[128,8]{1,0:T(8,128)S(1)}, f32[128,8]{1,0:T(8,128)S(1)}, u32[]{:S(2)}, u32[]{:S(2)}) collective-permute-start(f32[128,8]{1,0:T(8,128)S(1)} %get-tuple-element.18), channel_id=1, source_target_pairs={{0,32},{32,0},{64,96},{96,64},{128,160},{160,128},{192,224},{224,1... | collective-permute-start | bytes 12296 | tf_op jit(solution)/shard_map/ppermute | solution.py:119
  369.3 34.4 %collective-permute-start.1 = (f32[128,8]{1,0:T(8,128)S(1)}, f32[128,8]{1,0:T(8,128)S(1)}, u32[]{:S(2)}, u32[]{:S(2)}) collective-permute-start(f32[128,8]{1,0:T(8,128)S(1)} %add.130), channel_id=1, source_target_pairs={{0,64},{32,96},{64,0},{96,32},{128,192},{160,224},{192,128},{224,1... | collective-permute-start | bytes 12296 | tf_op jit(solution)/shard_map/ppermute | solution.py:119
  398.5 12.7 %copy-start.1 = (bf16[1,1024,640]{2,1,0:T(8,128)(2,1)S(1)}, bf16[1,1024,640]{2,1,0:T(8,128)(2,1)}, u32[]{:S(2)}) copy-start(bf16[1,1024,640]{2,1,0:T(8,128)(2,1)} %param.15) | copy-start | bytes 3932164
  403.7 6.8 %collective-permute-start.2 = (f32[128,8]{1,0:T(8,128)S(1)}, f32[128,8]{1,0:T(8,128)S(1)}, u32[]{:S(2)}, u32[]{:S(2)}) collective-permute-start(f32[128,8]{1,0:T(8,128)S(1)} %add.131), channel_id=1, source_target_pairs={{0,128},{32,160},{64,192},{96,224},{128,0},{160,32},{192,64},{224,... | collective-permute-start | bytes 12296 | tf_op jit(solution)/shard_map/ppermute | solution.py:119
  (2 other events, 5.4 us)
Sparse Core Ops, SparseCore 0:
  123.0 96.0 all-reduce.4
